TPU v7x, 16 devices: a 4x2x1 block of a 4x4x8 slice. The times are simulated.
16 devices in a mesh: rep: 4 (over y, z, core), dp: 4 (over x).
Axes of the slice: x: 4, y: 2, z: 1, core: 2. Of those that a mesh axis runs over, the one named last changes fastest.
The devices are a block of a 4x4x8 slice.
Arguments:
- x: bfloat16 [16, 4096, 640], P(('rep', 'dp')), parts along dimension 0
- dy: bfloat16 [16, 4096, 640], P(('rep', 'dp')), parts along dimension 0
- w_gate: bfloat16 [2, 640, 2048], replicated
- w_up: bfloat16 [2, 640, 2048], replicated
- w_down: bfloat16 [2, 2048, 640], replicated
- m_w_gate: float32 [2, 640, 2048], P(None, 'dp')
- m_w_up: float32 [2, 640, 2048], P(None, 'dp')
- m_w_down: float32 [2, 2048, 640], P(None, 'dp')
- v_w_gate: float32 [2, 640, 2048], P(None, 'dp')
- v_w_up: float32 [2, 640, 2048], P(None, 'dp')
- v_w_down: float32 [2, 2048, 640], P(None, 'dp')
Outputs:
- output 1: bfloat16 [8, 640, 2048], P('rep'), parts along dimension 0
- output 2: bfloat16 [8, 640, 2048], P('rep'), parts along dimension 0
- output 3: bfloat16 [8, 2048, 640], P('rep'), parts along dimension 0
- output 4: float32 [8, 640, 2048], P('rep', 'dp'), parts along dimension 0
- output 5: float32 [8, 640, 2048], P('rep', 'dp'), parts along dimension 0
- output 6: float32 [8, 2048, 640], P('rep', 'dp'), parts along dimension 0
- output 7: float32 [8, 640, 2048], P('rep', 'dp'), parts along dimension 0
- output 8: float32 [8, 640, 2048], P('rep', 'dp'), parts along dimension 0
- output 9: float32 [8, 2048, 640], P('rep', 'dp'), parts along dimension 0
There are 4 independent parts. A program takes and returns all parts, laid end to end along the dimension named above; an argument that names none is the same for every part.
All inputs are finite; a program needn't handle non-finite values.
Results may differ from a plain program's by a relative error of at most 0.022.
Values are sent between devices in bfloat16 or wider.
A program may use at most 768 MiB of HBM per device.

v0:
```python
import jax
import jax.numpy as jnp
from jax import lax

NAMES = ("w_gate", "w_up", "w_down")


def matmul(a, w):
    return jnp.dot(a, w, preferred_element_type=jnp.float32).astype(jnp.bfloat16)


def normed(h):
    wide = h.astype(jnp.float32)
    scale = lax.rsqrt(jnp.mean(wide**2, -1, keepdims=True) + 1e-6)
    return (wide * scale).astype(jnp.bfloat16)


def layer(h, w):
    a = normed(h)
    gate = jnp.dot(a, w["w_gate"], preferred_element_type=jnp.float32)
    up = jnp.dot(a, w["w_up"], preferred_element_type=jnp.float32)
    return h + matmul((jax.nn.silu(gate) * up).astype(jnp.bfloat16), w["w_down"])


def adamw(w, m, v, g):
    m = 0.9 * m + 0.1 * g
    v = 0.95 * v + 0.05 * g * g
    step = m * lax.rsqrt(v + 1e-8) + 0.1 * w
    return (w - 0.02 * step).astype(jnp.bfloat16), m, v


def clipped(gradients, sum_of_squares, count):
    factor = jnp.minimum(1.0, 0.5 * lax.rsqrt(sum_of_squares / count + 1e-30))
    return [g * factor for g in gradients]


def stack(weights, h):
    for number in range(weights["w_gate"].shape[0]):
        h = layer(h, {name: w[number] for name, w in weights.items()})
    return h


def solution(mesh):
    groups = mesh.shape["rep"]

    def step(x, dy, *arrays):
        weights, m, v = (arrays[i : i + 3] for i in (0, 3, 6))
        x, dy = (t.reshape(groups, -1, *t.shape[1:]) for t in (x, dy))

        def of_a_group(x, dy):
            _, back = jax.vjp(lambda w: stack(w, x), dict(zip(NAMES, weights, strict=True)))
            by_weights = back(dy)[0]
            gradients = [by_weights[name].astype(jnp.float32) for name in NAMES]
            gradients = clipped(gradients, sum(jnp.sum(g * g) for g in gradients), sum(g.size for g in gradients))
            new = [adamw(w.astype(jnp.float32), m, v, g) for w, m, v, g in zip(weights, m, v, gradients, strict=True)]
            return tuple(one[which] for which in range(3) for one in new)

        return tuple(t.reshape(-1, *t.shape[2:]) for t in jax.vmap(of_a_group)(x, dy))

    return step
```

profile of v0, /device:TPU:112, one launch (start us, length us, event | category | flops | bytes accessed | tf_op | source)
XLA Modules:
  0.0 808.1 jit_solution(10284077432148492879)
XLA Ops:
  10.9 7.9 copy
  18.8 22.0 %fusion.122 = f32[4096,2048]{1,0:T(8,128)} fusion(bf16[2,640,2048]{2,1,0:T(8,128)(2,1)} %param, bf16[1,4096,640]{2,1,0:T(8,128)(2,1)} %param.2, f32[4096]{0:T(1024)S(1)} %add_rsqrt_fusion), kind=kOutput, calls=%fused_computation.133 | convolution fusion | flops 10745282560 | bytes 41435136 | tf_op jit(solution)/vmap(jvp())/dot_general | solution.py:20
  40.8 19.0 %fusion.120 = f32[4096,2048]{1,0:T(8,128)} fusion(bf16[2,640,2048]{2,1,0:T(8,128)(2,1)} %param.3, bf16[1,4096,640]{2,1,0:T(8,128)(2,1)S(1)} %bitcast.363, f32[4096]{0:T(1024)S(1)} %add_rsqrt_fusion), kind=kOutput, calls=%fused_computation.131 | convolution fusion | flops 10745282560 | bytes 41435136 | tf_op jit(solution)/vmap(jvp())/dot_general | solution.py:21
  59.8 27.5 %fusion.26 = bf16[4096,2048]{1,0:T(8,128)(2,1)} fusion(f32[4096,2048]{1,0:T(8,128)} %fusion.120, f32[4096,2048]{1,0:T(8,128)} %fusion.122), kind=kLoop, calls=%fused_computation.39 | loop fusion | flops 50331648 | bytes 83886080
  87.4 19.0 %fusion.39 = (f32[4096]{0:T(1024)S(1)}, bf16[1,1,4096,640]{2,3,1,0:T(8,128)(2,1)}) fusion(bf16[4096,2048]{1,0:T(8,128)(2,1)} %fusion.26, bf16[2,2048,640]{2,1,0:T(8,128)(2,1)} %param.4, bf16[1,4096,640]{1,2,0:T(8,128)(2,1)} %copy), kind=kOutput, calls=%fused_computation.56 | convolution fusion | flops 10750521344 | bytes 29900800 | tf_op jit(solution)/vmap(jvp())/dot_general | solution.py:9
  106.9 22.2 %fusion.81 = f32[4096,2048]{1,0:T(8,128)} fusion(bf16[1,1,4096,640]{2,3,1,0:T(8,128)(2,1)} %get-tuple-element.10, f32[4096]{0:T(1024)S(1)} %bitcast.372, bf16[2,640,2048]{2,1,0:T(8,128)(2,1)} %param), kind=kOutput, calls=%fused_computation.83 | convolution fusion | flops 10745282560 | bytes 41435136 | tf_op jit(solution)/vmap(jvp())/dot_general | solution.py:20
  129.1 18.9 %fusion.83 = f32[4096,2048]{1,0:T(8,128)} fusion(bf16[1,1,4096,640]{2,3,1,0:T(8,128)(2,1)S(1)} %copy-done.2, f32[4096]{0:T(1024)S(1)} %bitcast.373, bf16[2,640,2048]{2,1,0:T(8,128)(2,1)} %param.3), kind=kOutput, calls=%fused_computation.84 | convolution fusion | flops 10745282560 | bytes 41435136 | tf_op jit(solution)/vmap(jvp())/dot_general | solution.py:21
  148.1 19.9 %convolution_convert_fusion.1 = bf16[4096,2048]{1,0:T(8,128)(2,1)} fusion(bf16[1,4096,640]{2,1,0:T(8,128)(2,1)} %param.5, bf16[2,2048,640]{2,1,0:T(8,128)(2,1)} %param.4), kind=kOutput, calls=%fused_computation.48 | convolution fusion | flops 10745806848 | bytes 24641536 | tf_op jit(solution)/vmap(transpose(jvp()))/dot_general | solution.py:9
  168.0 8.0 copy.1
  175.9 27.1 %fusion.6 = bf16[4096,2048]{1,0:T(8,128)(2,1)S(1)} fusion(f32[4096,2048]{1,0:T(8,128)} %fusion.81, f32[4096,2048]{1,0:T(8,128)} %fusion.83, bf16[4096,2048]{1,0:T(8,128)(2,1)} %convolution_convert_fusion.1), kind=kLoop, calls=%fused_computation.11 | loop fusion | flops 100663296 | bytes 100663296
  203.1 5.7 copy-done
  208.8 19.2 %convolution_convert_fusion.3 = bf16[4096,640]{0,1:T(8,128)(2,1)} fusion(bf16[4096,2048]{1,0:T(8,128)(2,1)S(1)} %fusion.6, bf16[2,640,2048]{2,1,0:T(8,128)(2,1)} %param), kind=kOutput, calls=%fused_computation.62 | convolution fusion | flops 10737418240 | bytes 24641536 | tf_op jit(solution)/vmap(transpose(jvp()))/dot_general | solution.py:20
  228.0 26.0 %fusion.41 = (f32[4096]{0:T(1024)S(1)}, bf16[1,1,4096,640]{2,3,1,0:T(8,128)(2,1)}) fusion(bf16[1,1,4096,640]{2,3,1,0:T(8,128)(2,1)} %get-tuple-element.10, bf16[4096,640]{0,1:T(8,128)(2,1)} %convolution_convert_fusion.3, bf16[2,640,2048]{2,1,0:T(8,128)(2,1)} %param.3, bf16[4096,2048]{1,0:T(8,128)(2,1)} %convolution_convert_fusion.1, f32[4096,2048]{1,0:T(8,128)} %fusion.81), kind=kOutput, calls=%fused_computation.58 | convolution fusion | flops 10803474432 | bytes 68698112 | tf_op jit(solution)/vmap(transpose(jvp()))/dot_general | solution.py:21
  254.1 11.9 %fusion.56 = bf16[4096,640]{0,1:T(8,128)(2,1)} fusion(bf16[1,1,4096,640]{2,3,1,0:T(8,128)(2,1)} %get-tuple-element.10, bf16[1,1,4096,640]{2,3,1,0:T(8,128)(2,1)} %get-tuple-element.12, bf16[1,4096,640]{1,2,0:T(8,128)(2,1)} %copy.1, f32[4096]{0:T(1024)S(1)} %bitcast.371, f32[4096]{0:T(1024)S(1)} %bitcast.374), kind=kLoop, calls=%fused_computation.70 | loop fusion | flops 18350080 | bytes 21004288
  266.0 18.7 %convolution_bitcast_fusion = f32[1,2048,640]{2,1,0:T(8,128)} fusion(bf16[4096,2048]{1,0:T(8,128)(2,1)} %fusion.26, bf16[4096,640]{0,1:T(8,128)(2,1)} %fusion.56), kind=kOutput, calls=%fused_computation.80 | convolution fusion | flops 10737418240 | bytes 27262976 | tf_op jit(solution)/vmap(transpose(jvp()))/dot_general | solution.py:9
  284.8 27.7 %fusion.62 = f32[1,2048,640]{2,1,0:T(8,128)} fusion(bf16[1,4096,640]{2,1,0:T(8,128)(2,1)} %param.5, f32[4096,2048]{1,0:T(8,128)} %fusion.83, f32[4096,2048]{1,0:T(8,128)} %fusion.81), kind=kOutput, calls=%fused_computation.77 | convolution fusion | flops 10787749888 | bytes 77594624 | tf_op jit(solution)/vmap(transpose(jvp()))/dot_general | solution.py:9
  312.7 20.0 %convolution_convert_fusion = bf16[4096,2048]{1,0:T(8,128)(2,1)} fusion(bf16[4096,640]{0,1:T(8,128)(2,1)} %fusion.56, bf16[2,2048,640]{2,1,0:T(8,128)(2,1)} %param.4), kind=kOutput, calls=%fused_computation.47 | convolution fusion | flops 10745806848 | bytes 24641536 | tf_op jit(solution)/vmap(transpose(jvp()))/dot_general | solution.py:9
  332.7 23.1 %fusion.70 = f32[1,640,2048]{2,1,0:T(8,128)} fusion(bf16[4096,2048]{1,0:T(8,128)(2,1)} %convolution_convert_fusion, f32[4096,2048]{1,0:T(8,128)} %fusion.122, bf16[1,4096,640]{1,2,0:T(8,128)(2,1)} %copy, f32[4096]{0:T(1024)S(1)} %copy-done.9), kind=kOutput, calls=%fused_computation.79 | convolution fusion | flops 10795614208 | bytes 60833792 | tf_op jit(solution)/vmap(transpose(jvp()))/dot_general | solution.py:21
  356.5 23.5 %fusion.67 = f32[1,640,2048]{2,1,0:T(8,128)} fusion(bf16[4096,2048]{1,0:T(8,128)(2,1)} %convolution_convert_fusion.1, f32[4096,2048]{1,0:T(8,128)} %fusion.81, bf16[1,1,4096,640]{2,3,1,0:T(8,128)(2,1)} %get-tuple-element.10, f32[4096]{0:T(1024)S(1)} %bitcast.375), kind=kOutput, calls=%fused_computation.78 | convolution fusion | flops 10795614208 | bytes 60833792 | tf_op jit(solution)/vmap(transpose(jvp()))/dot_general | solution.py:21
  380.2 36.1 %fusion.75 = f32[1,640,2048]{2,1,0:T(8,128)} fusion(f32[4096,2048]{1,0:T(8,128)} %fusion.122, f32[4096,2048]{1,0:T(8,128)} %fusion.120, bf16[4096,2048]{1,0:T(8,128)(2,1)} %convolution_convert_fusion, bf16[1,4096,640]{1,2,0:T(8,128)(2,1)} %copy, f32[4096]{0:T(1024)S(1)} %copy-done.9), kind=kOutput, calls=%fused_computation.82 | convolution fusion | flops 10837557248 | bytes 94388224 | tf_op jit(solution)/vmap(transpose(jvp()))/dot_general | solution.py:20
  416.4 17.7 %convolution_bitcast_fusion.1 = f32[1,640,2048]{2,1,0:T(8,128)} fusion(bf16[4096,2048]{1,0:T(8,128)(2,1)} %copy-done, bf16[1,1,4096,640]{2,3,1,0:T(8,128)(2,1)} %get-tuple-element.10, f32[4096]{0:T(1024)S(1)} %bitcast.376), kind=kOutput, calls=%fused_computation.81 | convolution fusion | flops 10745282560 | bytes 27279360 | tf_op jit(solution)/vmap(transpose(jvp()))/dot_general | solution.py:20
  447.2 51.8 %reduce-scatter.23.cloned.1.call-done = f32[1,160,2048]{2,1,0:T(8,128)} async-done(((f32[1,640,2048]{2,1,0:T(8,128)}), f32[1,160,2048]{2,1,0:T(8,128)}) %reduce-scatter.23.cloned.1.call-update) | async-done | bytes 1310736
  501.7 51.1 %reduce-scatter.21.cloned.1.call-done = f32[1,160,2048]{2,1,0:T(8,128)} async-done(((f32[1,640,2048]{2,1,0:T(8,128)}), f32[1,160,2048]{2,1,0:T(8,128)}) %reduce-scatter.21.cloned.1.call-update) | async-done | bytes 1310736
  554.2 52.4 %reduce-scatter.19.cloned.1.call-done = f32[1,160,2048]{2,1,0:T(8,128)} async-done(((f32[1,640,2048]{2,1,0:T(8,128)}), f32[1,160,2048]{2,1,0:T(8,128)}) %reduce-scatter.19.cloned.1.call-update) | async-done | bytes 1310736
  611.2 9.7 %all-reduce.16 = f32[1]{0:T(128)} all-reduce(f32[1]{0:T(128)} %bitcast.50), channel_id=5, replica_groups=mesh['rep'=4,'dp'=4] {'dp'}, use_global_device_ids=true, to_apply=%region_3.4.clone | all-reduce | flops 1 | bytes 8 | tf_op jit(solution)/vmap()/reduce_sum | solution.py:54
  621.6 5.5 fusion.138
  627.3 5.4 fusion.139
  632.9 5.4 fusion.140
  638.4 41.2 %all-gather.14.cloned.1.call-done = bf16[1,2,2048,640]{3,2,1,0:T(8,128)(2,1)} async-done(((bf16[1,2,512,640]{3,2,1,0:T(8,128)(2,1)}), bf16[1,2,2048,640]{3,2,1,0:T(8,128)(2,1)}) %all-gather.14.cloned.1.call-update) | async-done | bytes 5242896 | tf_op jit(solution)/reshape | solution.py:58
  679.6 55.5 %all-gather.12.cloned.1.call-done = bf16[1,2,640,2048]{3,2,1,0:T(8,128)(2,1)} async-done(((bf16[1,2,160,2048]{3,2,1,0:T(8,128)(2,1)}), bf16[1,2,640,2048]{3,2,1,0:T(8,128)(2,1)}) %all-gather.12.cloned.1.call-update) | async-done | bytes 5242896 | tf_op jit(solution)/reshape | solution.py:58
  735.0 55.5 %all-gather.10.cloned.1.call-done = bf16[1,2,640,2048]{3,2,1,0:T(8,128)(2,1)} async-done(((bf16[1,2,160,2048]{3,2,1,0:T(8,128)(2,1)}), bf16[1,2,640,2048]{3,2,1,0:T(8,128)(2,1)}) %all-gather.10.cloned.1.call-update) | async-done | bytes 5242896 | tf_op jit(solution)/reshape | solution.py:58
  790.5 6.2 copy.5
  (69 shorter events, 29.7 us)
Async XLA Ops:
  7.2 428.8 %reduce-scatter.29.cloned.1.call-start = ((), (), s32[]{:S(2)}) async-start(), calls=%async_computation.14 | async-start | bytes 6553600
  10.8 30.0 %slice-start = ((s8[5242880]{0:T(1024)(128)(4,1)}), s8[1048576]{0:T(1024)(128)(4,1)S(1)}, s32[]{:S(2)}) async-start(s8[5242880]{0:T(1024)(128)(4,1)} %bitcast.362), calls=%async_computation.15 | async-start | bytes 2097152
  18.8 22.0 %copy-start.8 = (f32[4096]{0:T(1024)}, f32[4096]{0:T(1024)S(1)}, u32[]{:S(2)}) copy-start(f32[4096]{0:T(1024)S(1)} %add_rsqrt_fusion) | copy-start | bytes 49156
  18.8 22.0 %slice-start.1 = ((s8[5242880]{0:T(1024)(128)(4,1)}), s8[4194304]{0:T(1024)(128)(4,1)S(1)}, s32[]{:S(2)}) async-start(s8[5242880]{0:T(1024)(128)(4,1)} %bitcast.362), calls=%async_computation.16 | async-start | bytes 8388608
  106.3 0.6 copy-start.4
  106.4 147.7 %copy-start.6 = (f32[1,1,4096]{2,1,0:T(1,128)}, f32[1,1,4096]{2,1,0:T(1,128)S(1)}, u32[]{:S(2)}) copy-start(f32[1,1,4096]{2,1,0:T(1,128)S(1)} %rsqrt.38) | copy-start | bytes 49156
  106.9 22.2 %copy-start.2 = (bf16[1,1,4096,640]{2,3,1,0:T(8,128)(2,1)S(1)}, bf16[1,1,4096,640]{2,3,1,0:T(8,128)(2,1)}, u32[]{:S(2)}) copy-start(bf16[1,1,4096,640]{2,3,1,0:T(8,128)(2,1)} %get-tuple-element.10) | copy-start | bytes 15728644
  203.0 5.7 copy-start
  228.0 26.0 %copy-start.5 = (f32[4096]{0:T(1024)S(1)}, f32[4096]{0:T(1024)}, u32[]{:S(2)}) copy-start(f32[4096]{0:T(1024)} %copy-done.4) | copy-start | bytes 49156
  284.7 152.7 %reduce-scatter.27.cloned.1.call-start = ((), (), s32[]{:S(2)}) async-start(), calls=%async_computation.13 | async-start | bytes 6553600
  312.6 20.1 %copy-start.9 = (f32[4096]{0:T(1024)S(1)}, f32[4096]{0:T(1024)}, u32[]{:S(2)}) copy-start(f32[4096]{0:T(1024)} %copy-done.8) | copy-start | bytes 49156
  312.6 133.2 %reduce-scatter.25.cloned.1.call-start = ((), (), s32[]{:S(2)}) async-start(), calls=%async_computation.12 | async-start | bytes 6553600
  355.8 0.7 copy-start.7
  355.9 143.2 %reduce-scatter.23.cloned.1.call-start = ((), (), s32[]{:S(2)}) async-start(), calls=%async_computation.11 | async-start | bytes 6553600
  380.1 172.7 %reduce-scatter.21.cloned.1.call-start = ((), (), s32[]{:S(2)}) async-start(), calls=%async_computation.10 | async-start | bytes 6553600
  416.3 190.3 %reduce-scatter.19.cloned.1.call-start = ((), (), s32[]{:S(2)}) async-start(), calls=%async_computation.9 | async-start | bytes 6553600
  434.1 0.7 copy-start.10
  434.2 245.4 %all-gather.14.cloned.1.call-start = ((), (), s32[]{:S(2)}) async-start(), calls=%async_computation.8 | async-start | bytes 6553600 | tf_op jit(solution)/reshape | solution.py:58
  438.8 0.8 copy-start.1
  627.2 107.8 %all-gather.12.cloned.1.call-start = ((), (), s32[]{:S(2)}) async-start(), calls=%async_computation.7 | async-start | bytes 6553600 | tf_op jit(solution)/reshape | solution.py:58
  632.8 157.7 %all-gather.10.cloned.1.call-start = ((), (), s32[]{:S(2)}) async-start(), calls=%async_computation.6 | async-start | bytes 6553600 | tf_op jit(solution)/reshape | solution.py:58
  790.5 6.2 copy-start.3
  790.5 8.5 %slice-start.2 = ((s8[5242880]{0:T(1024)(128)(4,1)}), s8[4194304]{0:T(1024)(128)(4,1)S(1)}, s32[]{:S(2)}) async-start(s8[5242880]{0:T(1024)(128)(4,1)} %bitcast.364), calls=%async_computation.17 | async-start | bytes 8388608
  796.7 2.4 slice-start.3
Sparse Core Ops, SparseCore 0:
  284.9 54.1 reduce-scatter.28
  341.4 51.0 reduce-scatter.26
  394.8 51.0 reduce-scatter.24
  448.0 51.0 reduce-scatter.22
  501.8 51.0 reduce-scatter.20
  555.5 51.0 reduce-scatter.18
  627.4 52.1 all-gather.13
  681.7 53.2 all-gather.11
  737.2 53.2 all-gather.9
where the time goes:
time: 817 us; the launch traced here: 808 us
  matrix products  333 us (41%)
  waiting for transfers between devices  313 us (38%)
  other arithmetic  98.8 us (12%)
  local copies, waits for them, and re-layouts  35.7 us (4%)
  between operations  17.6 us (2%)
  blocking collectives  9.72 us (1%)
    unnamed x15, waiting for transfers between devices  161 us
    reshape x3, waiting for transfers between devices, step(): t.reshape(-1, *t.shape[2:])  152 us
    dot_general x5, matrix products, layer(): gate = jnp.dot(a, w['w_gate'], preferred_element_type=jnp.float32)  117 us
    dot_general x5, matrix products, layer(): up = jnp.dot(a, w['w_up'], preferred_element_type=jnp.float32)  111 us
    dot_general x5, matrix products, matmul(): jnp.dot(a, w, preferred_element_type=jnp.float32).astype(jnp.bfloat16)  105 us
    unnamed x5, other arithmetic  66.6 us
    unnamed x35, local copies, waits for them, and re-layouts  35 us
    reshape x3, other arithmetic, step(): t.reshape(-1, *t.shape[2:])  16.4 us
  transfers between devices with their start and end apart: 9, of which 7 were waited for; matrix products, arithmetic and copies ran while one was open for 21% of the time, Pallas kernels for 0%

commit v1 on v0

v1 whole, which is shorter than its diff:
```python
import functools

import jax
import jax.numpy as jnp
from jax import lax
from jax.experimental import pallas as pl
from jax.experimental.pallas import tpu as pltpu
from jax.sharding import PartitionSpec as P

F32, BF16 = jnp.float32, jnp.bfloat16
VMEM_BYTES = 66_000_000
NN = (((1,), (0,)), ((), ()))
NT = (((1,), (1,)), ((), ()))
TN = (((0,), (0,)), ((), ()))


def dot(a, b, dims=NN):
    return lax.dot_general(a, b, dims, preferred_element_type=F32)


def params(**more):
    return pltpu.CompilerParams(vmem_limit_bytes=VMEM_BYTES, **more)


def cost(flops, nbytes):
    return pl.CostEstimate(flops=flops, bytes_accessed=nbytes, transcendentals=0)


def tokens_spec(tile, width):
    return pl.BlockSpec((tile, width), lambda i: (i, 0))


def weight_spec(w, layer):
    return pl.BlockSpec((None, *w.shape[1:]), lambda i: (layer, 0, 0), pipeline_mode=pl.Buffered(1))


def scale_of(wide):
    return lax.rsqrt(jnp.mean(wide * wide, -1, keepdims=True) + 1e-6)


def gated(gate, up):
    sig = 0.5 * jnp.tanh(0.5 * gate) + 0.5
    act = gate * sig
    return act, up * (sig + act * (1.0 - sig)), (act * up).astype(BF16)


def first_kernel(chunk, x_ref, wg, wu, wd, act_ref, slope_ref, hid_ref, h1_ref, a_ref):
    wide = x_ref[...].astype(F32)
    a = (wide * scale_of(wide)).astype(BF16)
    a_ref[...] = a
    for c in range(0, wg.shape[1], chunk):
        at = pl.ds(c, chunk)
        act, slope, hid = gated(dot(a, wg[:, at]), dot(a, wu[:, at]))
        act_ref[:, at] = act
        slope_ref[:, at] = slope
        hid_ref[:, at] = hid
    y = dot(hid_ref[...], wd[...]).astype(BF16)
    h1_ref[...] = (wide + y.astype(F32)).astype(BF16)


def first(x, wg, wu, wd, tile=512, chunk=512):
    t, d = x.shape
    f = wg.shape[2]
    return pl.pallas_call(
        functools.partial(first_kernel, chunk),
        grid=(t // tile,),
        in_specs=[tokens_spec(tile, d), weight_spec(wg, 0), weight_spec(wu, 0), weight_spec(wd, 0)],
        out_specs=[tokens_spec(tile, f)] * 3 + [tokens_spec(tile, d)] * 2,
        out_shape=[
            jax.ShapeDtypeStruct((t, f), F32),
            jax.ShapeDtypeStruct((t, f), F32),
            jax.ShapeDtypeStruct((t, f), BF16),
            jax.ShapeDtypeStruct((t, d), BF16),
            jax.ShapeDtypeStruct((t, d), BF16),
        ],
        compiler_params=params(),
        cost_estimate=cost(6 * t * d * f, 10 * t * f),
        name="first",
    )(x, wg, wu, wd)


def second_kernel(chunk, h_ref, dy_ref, wg, wu, wd, hid_ref, dgate_ref, dup_ref, a_ref):
    wide = h_ref[...].astype(F32)
    a = (wide * scale_of(wide)).astype(BF16)
    a_ref[...] = a
    dy = dy_ref[...]
    for c in range(0, wg.shape[1], chunk):
        at = pl.ds(c, chunk)
        act, slope, hid = gated(dot(a, wg[:, at]), dot(a, wu[:, at]))
        hid_ref[:, at] = hid
        dhid = dot(dy, wd[at, :], NT).astype(BF16).astype(F32)
        dgate_ref[:, at] = (dhid * slope).astype(BF16)
        dup_ref[:, at] = (dhid * act).astype(BF16)


def second(h, dy, wg, wu, wd, tile=512, chunk=512):
    t, d = h.shape
    f = wg.shape[2]
    return pl.pallas_call(
        functools.partial(second_kernel, chunk),
        grid=(t // tile,),
        in_specs=[tokens_spec(tile, d)] * 2 + [weight_spec(wg, 1), weight_spec(wu, 1), weight_spec(wd, 1)],
        out_specs=[tokens_spec(tile, f)] * 3 + [tokens_spec(tile, d)],
        out_shape=[jax.ShapeDtypeStruct((t, f), BF16)] * 3 + [jax.ShapeDtypeStruct((t, d), BF16)],
        compiler_params=params(),
        cost_estimate=cost(6 * t * d * f, 6 * t * f),
        name="second",
    )(h, dy, wg, wu, wd)


def third_kernel(chunk, dgate_ref, dup_ref, h_ref, dy_ref, act_ref, slope_ref, wg, wu, wd, dh_ref, dgate0_ref, dup0_ref):
    da = dot(dgate_ref[...], wg[...], NT).astype(BF16) + dot(dup_ref[...], wu[...], NT).astype(BF16)
    da = da.astype(F32)
    wide = h_ref[...].astype(F32)
    scale = scale_of(wide)
    along = jnp.mean(da * wide, -1, keepdims=True)
    dn = da * scale - wide * (scale * scale * scale * along)
    dh = (dy_ref[...].astype(F32) + dn.astype(BF16).astype(F32)).astype(BF16)
    dh_ref[...] = dh
    for c in range(0, wd.shape[0], chunk):
        at = pl.ds(c, chunk)
        dhid = dot(dh, wd[at, :], NT).astype(BF16).astype(F32)
        dgate0_ref[:, at] = (dhid * slope_ref[:, at]).astype(BF16)
        dup0_ref[:, at] = (dhid * act_ref[:, at]).astype(BF16)


def third(dgate, dup, h, dy, act, slope, wg, wu, wd, tile=512, chunk=512):
    t, d = h.shape
    f = wg.shape[2]
    return pl.pallas_call(
        functools.partial(third_kernel, chunk),
        grid=(t // tile,),
        in_specs=[tokens_spec(tile, f)] * 2
        + [tokens_spec(tile, d)] * 2
        + [tokens_spec(tile, f)] * 2
        + [weight_spec(wg, 1), weight_spec(wu, 1), weight_spec(wd, 0)],
        out_specs=[tokens_spec(tile, d)] + [tokens_spec(tile, f)] * 2,
        out_shape=[jax.ShapeDtypeStruct((t, d), BF16)] + [jax.ShapeDtypeStruct((t, f), BF16)] * 2,
        compiler_params=params(),
        cost_estimate=cost(6 * t * d * f, 16 * t * f),
        name="third",
    )(dgate, dup, h, dy, act, slope, wg, wu, wd)


def outer_kernel(flip, a_ref, b_ref, o_ref):
    out = dot(a_ref[...], b_ref[...], TN)
    o_ref[...] = (out.T if flip else out).astype(BF16)


def outer(a, b, flip, name, tile=512):
    t, d = a.shape
    f = b.shape[1]
    return pl.pallas_call(
        functools.partial(outer_kernel, flip),
        grid=(f // tile,),
        in_specs=[
            pl.BlockSpec((t, d), lambda i: (0, 0), pipeline_mode=pl.Buffered(1)),
            pl.BlockSpec((t, tile), lambda i: (0, i)),
        ],
        out_specs=pl.BlockSpec((tile, d), lambda i: (i, 0)) if flip else pl.BlockSpec((d, tile), lambda i: (0, i)),
        out_shape=jax.ShapeDtypeStruct((f, d) if flip else (d, f), BF16),
        compiler_params=params(),
        cost_estimate=cost(2 * t * d * f, 2 * t * f),
        name=name,
    )(a, b)


def adamw(w, m, v, g):
    m = 0.9 * m + 0.1 * g
    v = 0.95 * v + 0.05 * g * g
    step = m * lax.rsqrt(v + 1e-8) + 0.1 * w
    return (w - 0.02 * step).astype(BF16), m, v


def solution(mesh):
    def scatter(dw):
        return lax.psum_scatter(dw, "dp", scatter_dimension=0, tiled=True)

    def body(x, dy, wg, wu, wd, *moments):
        m, v = moments[:3], moments[3:]
        x, dy = x[0], dy[0]
        act0, slope0, hid0, h1, a0 = first(x, wg, wu, wd)
        hid1, dgate1, dup1, a1 = second(h1, dy, wg, wu, wd)
        gd1 = scatter(outer(dy, hid1, True, "dwd1"))
        gg1 = scatter(outer(a1, dgate1, False, "dwg1"))
        gu1 = scatter(outer(a1, dup1, False, "dwu1"))
        dh1, dgate0, dup0 = third(dgate1, dup1, h1, dy, act0, slope0, wg, wu, wd)
        gd0 = scatter(outer(dh1, hid0, True, "dwd0"))
        gg0 = scatter(outer(a0, dgate0, False, "dwg0"))
        gu0 = scatter(outer(a0, dup0, False, "dwu0"))
        grads = [[t.astype(F32) for t in pair] for pair in ((gg0, gg1), (gu0, gu1), (gd0, gd1))]
        total = lax.psum(sum(jnp.sum(g * g) for pair in grads for g in pair), "dp")
        count = sum(w.size for w in (wg, wu, wd))
        factor = jnp.minimum(1.0, 0.5 * lax.rsqrt(total / count + 1e-30))
        me = lax.axis_index("dp")
        new = []
        for w, mw, vw, pair in zip((wg, wu, wd), m, v, grads, strict=True):
            g = jnp.stack(pair) * factor
            rows = mw.shape[1]
            mine = lax.dynamic_slice_in_dim(w, me * rows, rows, 1).astype(F32)
            nw, nm, nv = adamw(mine, mw, vw, g)
            new.append((lax.all_gather(nw, "dp", axis=1, tiled=True), nm, nv))
        return tuple(one[which] for which in range(3) for one in new)

    whole, rows = P(None, None, None), P(None, "dp", None)
    return jax.shard_map(
        body,
        mesh=mesh,
        in_specs=(P(("rep", "dp")),) * 2 + (whole,) * 3 + (rows,) * 6,
        out_specs=(P("rep"),) * 3 + (P("rep", "dp"),) * 6,
        check_vma=False,
    )
```

time: 817 us -> 580 us (0.71); the launches traced: 808 us -> 580 us
  matrix products: 333 us -> 0 us
  Pallas kernels: 0 us -> 260 us
  other arithmetic: 98.8 us -> 29.1 us
  waiting for transfers between devices: 313 us -> 249 us
  local copies, waits for them, and re-layouts: 35.7 us -> 14 us
    dot_general x15 -> x0, matrix products: 333 us -> none  [the longest x5 117 us: layer(): gate = jnp.dot(a, w['w_gate'], preferred_element_type=jnp.float32)]
    pallas_call x0 -> x9, Pallas kernels: none -> 260 us  [the longest x6 98.5 us: outer(): pl.pallas_call(functools.partial(outer_kernel, flip), grid=(f // tile,),...]
    unnamed x15 -> x9, waiting for transfers between devices: 161 us -> 0.48 us
    reshape x3 -> x0, waiting for transfers between devices: 152 us -> none  [step(): t.reshape(-1, *t.shape[2:])]
    all_gather x0 -> x3, waiting for transfers between devices: none -> 149 us  [body(): new.append((lax.all_gather(nw, 'dp', axis=1, tiled=True), nm, nv))]
    reduce_scatter x0 -> x6, waiting for transfers between devices: none -> 98.8 us  [scatter(): return lax.psum_scatter(dw, 'dp', scatter_dimension=0, tiled=True)]
    unnamed x5 -> x1, other arithmetic: 66.6 us -> 0.01 us
    unnamed x35 -> x25, local copies, waits for them, and re-layouts: 35 us -> 14 us
  transfers between devices with their start and end apart: 9 -> 9, of which waited for: 7 -> 7; matrix products, arithmetic and copies ran while one was open for 21% -> 4% of each run, Pallas kernels for 0% -> 14%
where the time goes in v1:
time: 580 us
  Pallas kernels  260 us (45%)
  waiting for transfers between devices  249 us (43%)
  other arithmetic  29.1 us (5%)
  between operations  18.6 us (3%)
  local copies, waits for them, and re-layouts  14 us (2%)
  blocking collectives  9.14 us (2%)
    all_gather x3, waiting for transfers between devices, body(): new.append((lax.all_gather(nw, 'dp', axis=1, tiled=True), nm, nv))  149 us
    reduce_scatter x6, waiting for transfers between devices, scatter(): return lax.psum_scatter(dw, 'dp', scatter_dimension=0, tiled=True)  98.8 us
    pallas_call x6, Pallas kernels, outer(): pl.pallas_call(functools.partial(outer_kernel, flip), grid=(f // tile,),...  98.5 us
    pallas_call x1, Pallas kernels, third(): pl.pallas_call(functools.partial(third_kernel, chunk), grid=(t // tile,),...  59.7 us
    pallas_call x1, Pallas kernels, second(): pl.pallas_call(functools.partial(second_kernel, chunk), grid=(t // tile,)...  51.9 us
    pallas_call x1, Pallas kernels, first(): pl.pallas_call(functools.partial(first_kernel, chunk), grid=(t // tile,),...  49.6 us
    convert_element_type x3, other arithmetic, adamw(): return ((w - 0.02 * step).astype(BF16), m, v)  15.1 us
    unnamed x25, local copies, waits for them, and re-layouts  14 us
  transfers between devices with their start and end apart: 9, of which 7 were waited for; matrix products, arithmetic and copies ran while one was open for 4% of the time, Pallas kernels for 14%

profile of v1, /device:TPU:112, one launch (start us, length us, event | category | flops | bytes accessed | tf_op | source)
XLA Modules:
  0.0 579.7 jit_solution(18109390144821552010)
XLA Ops:
  7.3 49.6 %first.1 = (f32[4096,2048]{1,0:T(8,128)}, f32[4096,2048]{1,0:T(8,128)}, bf16[4096,2048]{1,0:T(8,128)(2,1)}, bf16[4096,640]{1,0:T(8,128)(2,1)}, bf16[4096,640]{1,0:T(8,128)(2,1)}) custom-call(bf16[4096,640]{1,0:T(8,128)(2,1)} %bitcast.19, bf16[2,640,2048]{2,1,0:T(8,128)(2,1)} %wg.5, bf16[2,640,2048]{2,1,0:T(8,128)(2,1)} %wu.5, bf16[2,2048,640]{2,1,0:T(8,128)(2,1)} %wd.5), custom_call_target="tpu_custom_call" | custom-call | flops 32212254720 | bytes 83886080 | tf_op jit(solution)/shard_map/first/pallas_call | solution.py:64
  56.9 51.9 %second.1 = (bf16[4096,2048]{1,0:T(8,128)(2,1)}, bf16[4096,2048]{1,0:T(8,128)(2,1)}, bf16[4096,2048]{1,0:T(8,128)(2,1)}, bf16[4096,640]{1,0:T(8,128)(2,1)}) custom-call(bf16[4096,640]{1,0:T(8,128)(2,1)} %get-tuple-element.22.h_ref, bf16[4096,640]{1,0:T(8,128)(2,1)} %bitcast.14, bf16[2,640,2048]{2,1,0:T(8,128)(2,1)} %wg.5, bf16[2,640,2048]{2,1,0:T(8,128)(2,1)} %wu.5, ...), custom_call_target="tpu_custom_call" | custom-call | flops 32212254720 | bytes 50331648 | tf_op jit(solution)/shard_map/second/pallas_call | solution.py:99
  108.8 59.7 %third.1 = (bf16[4096,640]{1,0:T(8,128)(2,1)}, bf16[4096,2048]{1,0:T(8,128)(2,1)}, bf16[4096,2048]{1,0:T(8,128)(2,1)}) custom-call(bf16[4096,2048]{1,0:T(8,128)(2,1)} %get-tuple-element.23.dgate_ref.b_ref, bf16[4096,2048]{1,0:T(8,128)(2,1)} %get-tuple-element.24.dup_ref.b_ref, bf16[4096,640]{1,0:T(8,128)(2,1)} %get-tuple-element.22.h_ref, ...), custom_call_target="tpu_custom_call" | custom-call | flops 32212254720 | bytes 134217728 | tf_op jit(solution)/shard_map/third/pallas_call | solution.py:130
  168.5 16.3 %dwg0.1 = bf16[640,2048]{1,0:T(8,128)(2,1)} custom-call(bf16[4096,640]{1,0:T(8,128)(2,1)} %get-tuple-element.21.a_ref, bf16[4096,2048]{1,0:T(8,128)(2,1)} %get-tuple-element.27.b_ref), custom_call_target="tpu_custom_call" | custom-call | flops 10737418240 | bytes 16777216 | tf_op jit(solution)/shard_map/dwg0/pallas_call | solution.py:153
  184.9 16.3 %dwg1.1 = bf16[640,2048]{1,0:T(8,128)(2,1)} custom-call(bf16[4096,640]{1,0:T(8,128)(2,1)} %get-tuple-element.28.a_ref, bf16[4096,2048]{1,0:T(8,128)(2,1)} %get-tuple-element.23.dgate_ref.b_ref), custom_call_target="tpu_custom_call" | custom-call | flops 10737418240 | bytes 16777216 | tf_op jit(solution)/shard_map/dwg1/pallas_call | solution.py:153
  201.3 16.3 %dwu0.1 = bf16[640,2048]{1,0:T(8,128)(2,1)} custom-call(bf16[4096,640]{1,0:T(8,128)(2,1)} %get-tuple-element.21.a_ref, bf16[4096,2048]{1,0:T(8,128)(2,1)} %get-tuple-element.29.b_ref), custom_call_target="tpu_custom_call" | custom-call | flops 10737418240 | bytes 16777216 | tf_op jit(solution)/shard_map/dwu0/pallas_call | solution.py:153
  217.7 16.5 %dwu1.1 = bf16[640,2048]{1,0:T(8,128)(2,1)} custom-call(bf16[4096,640]{1,0:T(8,128)(2,1)} %get-tuple-element.28.a_ref, bf16[4096,2048]{1,0:T(8,128)(2,1)} %get-tuple-element.24.dup_ref.b_ref), custom_call_target="tpu_custom_call" | custom-call | flops 10737418240 | bytes 16777216 | tf_op jit(solution)/shard_map/dwu1/pallas_call | solution.py:153
  234.3 16.6 %dwd0.1 = bf16[2048,640]{1,0:T(8,128)(2,1)} custom-call(bf16[4096,640]{1,0:T(8,128)(2,1)} %get-tuple-element.30.a_ref, bf16[4096,2048]{1,0:T(8,128)(2,1)} %get-tuple-element.31.b_ref), custom_call_target="tpu_custom_call" | custom-call | flops 10737418240 | bytes 16777216 | tf_op jit(solution)/shard_map/dwd0/pallas_call | solution.py:153
  251.1 16.6 %dwd1.1 = bf16[2048,640]{1,0:T(8,128)(2,1)} custom-call(bf16[4096,640]{1,0:T(8,128)(2,1)} %bitcast.16, bf16[4096,2048]{1,0:T(8,128)(2,1)} %get-tuple-element.32.b_ref), custom_call_target="tpu_custom_call" | custom-call | flops 10737418240 | bytes 16777216 | tf_op jit(solution)/shard_map/dwd1/pallas_call | solution.py:153
  267.8 2.0 fusion.12
  269.8 2.0 fusion.13
  273.1 9.7 %reduce-scatter.11.cloned.1.call-done = bf16[160,2048]{1,0:T(8,128)(2,1)} async-done(((bf16[640,2048]{1,0:T(8,128)(2,1)}), bf16[160,2048]{1,0:T(8,128)(2,1)}) %reduce-scatter.11.cloned.1.call-update) | async-done | bytes 655376 | tf_op jit(solution)/shard_map/reduce_scatter | solution.py:177
  282.8 2.0 fusion.14
  285.5 29.7 %reduce-scatter.13.cloned.1.call-done = bf16[160,2048]{1,0:T(8,128)(2,1)} async-done(((bf16[640,2048]{1,0:T(8,128)(2,1)}), bf16[160,2048]{1,0:T(8,128)(2,1)}) %reduce-scatter.13.cloned.1.call-update) | async-done | bytes 655376 | tf_op jit(solution)/shard_map/reduce_scatter | solution.py:177
  315.2 2.0 fusion.15
  317.9 29.7 %reduce-scatter.15.cloned.1.call-done = bf16[512,640]{1,0:T(8,128)(2,1)} async-done(((bf16[2048,640]{1,0:T(8,128)(2,1)}), bf16[512,640]{1,0:T(8,128)(2,1)}) %reduce-scatter.15.cloned.1.call-update) | async-done | bytes 655376 | tf_op jit(solution)/shard_map/reduce_scatter | solution.py:177
  347.6 2.0 fusion.16
  350.3 29.7 %reduce-scatter.17.cloned.1.call-done = bf16[512,640]{1,0:T(8,128)(2,1)} async-done(((bf16[2048,640]{1,0:T(8,128)(2,1)}), bf16[512,640]{1,0:T(8,128)(2,1)}) %reduce-scatter.17.cloned.1.call-update) | async-done | bytes 655376 | tf_op jit(solution)/shard_map/reduce_scatter | solution.py:177
  380.0 2.1 fusion.17
  382.7 9.1 %psum.7 = f32[]{:T(128)} all-reduce(f32[]{:T(128)S(6)} %add.83), channel_id=1, replica_groups=mesh['rep'=4,'dp'=4] {'dp'}, use_global_device_ids=true, to_apply=%region_12.0 | all-reduce | flops 1 | bytes 8 | tf_op jit(solution)/shard_map/psum | solution.py:192
  392.6 1.2 convert_bitcast_fusion.1
  393.9 5.1 fusion.8
  399.3 0.8 copy-done.4
  401.0 5.0 fusion.5
  406.3 0.8 copy-done.2
  408.0 5.0 fusion.2
  413.0 38.3 %all-gather.8.cloned.1.call-done = bf16[2,2048,640]{2,1,0:T(8,128)(2,1)} async-done(((bf16[2,512,640]{2,1,0:T(8,128)(2,1)}), bf16[2,2048,640]{2,1,0:T(8,128)(2,1)}) %all-gather.8.cloned.1.call-update) | async-done | bytes 5242896 | tf_op jit(solution)/shard_map/all_gather | solution.py:202
  451.4 55.5 %all-gather.6.cloned.1.call-done = bf16[2,640,2048]{2,1,0:T(8,128)(2,1)} async-done(((bf16[2,160,2048]{2,1,0:T(8,128)(2,1)}), bf16[2,640,2048]{2,1,0:T(8,128)(2,1)}) %all-gather.6.cloned.1.call-update) | async-done | bytes 5242896 | tf_op jit(solution)/shard_map/all_gather | solution.py:202
  506.8 55.5 %all-gather.4.cloned.1.call-done = bf16[2,640,2048]{2,1,0:T(8,128)(2,1)} async-done(((bf16[2,160,2048]{2,1,0:T(8,128)(2,1)}), bf16[2,640,2048]{2,1,0:T(8,128)(2,1)}) %all-gather.4.cloned.1.call-update) | async-done | bytes 5242896 | tf_op jit(solution)/shard_map/all_gather | solution.py:202
  562.3 6.2 %copy.23 = bf16[2,640,2048]{2,1,0:T(8,128)(2,1)} copy(bf16[2,640,2048]{2,1,0:T(8,128)(2,1)} %all-gather.4.cloned.1.call-done) | data formatting | bytes 10485760
  568.5 2.4 copy.24
  570.8 2.4 copy.25
  (46 shorter events, 3.3 us)
Async XLA Ops:
  7.2 260.6 %reduce-scatter.7.cloned.1.call-start = ((), (), s32[]{:S(2)}) async-start(), calls=%async_computation.6 | async-start | bytes 3276800 | tf_op jit(solution)/shard_map/reduce_scatter | solution.py:177
  184.8 85.0 %reduce-scatter.9.cloned.1.call-start = ((), (), s32[]{:S(2)}) async-start(), calls=%async_computation.7 | async-start | bytes 3276800 | tf_op jit(solution)/shard_map/reduce_scatter | solution.py:177
  201.2 81.6 %reduce-scatter.11.cloned.1.call-start = ((), (), s32[]{:S(2)}) async-start(), calls=%async_computation.8 | async-start | bytes 3276800 | tf_op jit(solution)/shard_map/reduce_scatter | solution.py:177
  217.6 97.6 %reduce-scatter.13.cloned.1.call-start = ((), (), s32[]{:S(2)}) async-start(), calls=%async_computation.9 | async-start | bytes 3276800 | tf_op jit(solution)/shard_map/reduce_scatter | solution.py:177
  234.3 113.3 %reduce-scatter.15.cloned.1.call-start = ((), (), s32[]{:S(2)}) async-start(), calls=%async_computation.10 | async-start | bytes 3276800 | tf_op jit(solution)/shard_map/reduce_scatter | solution.py:177
  251.0 129.0 %reduce-scatter.17.cloned.1.call-start = ((), (), s32[]{:S(2)}) async-start(), calls=%async_computation.11 | async-start | bytes 3276800 | tf_op jit(solution)/shard_map/reduce_scatter | solution.py:177
  267.7 183.7 %all-gather.8.cloned.1.call-start = ((), (), s32[]{:S(2)}) async-start(), calls=%async_computation.14 | async-start | bytes 6553600 | tf_op jit(solution)/shard_map/all_gather | solution.py:202
  317.9 76.0 %copy-start.6 = (f32[2,512,640]{2,1,0:T(8,128)S(1)}, f32[2,512,640]{2,1,0:T(8,128)}, u32[]{:S(2)}) copy-start(f32[2,512,640]{2,1,0:T(8,128)} %param.21) | copy-start | bytes 7864324
  380.0 13.8 %copy-start.5 = (bf16[512,640]{1,0:T(8,128)(2,1)S(1)}, bf16[512,640]{1,0:T(8,128)(2,1)}, u32[]{:S(2)}) copy-start(bf16[512,640]{1,0:T(8,128)(2,1)} %reduce-scatter.17.cloned.1.call-done) | copy-start | bytes 1966084
  393.9 5.2 copy-start.3
  399.0 1.1 copy-start.4
  399.0 107.8 %all-gather.6.cloned.1.call-start = ((), (), s32[]{:S(2)}) async-start(), calls=%async_computation.13 | async-start | bytes 6553600 | tf_op jit(solution)/shard_map/all_gather | solution.py:202
  399.1 1.8 copy-start.7
  401.0 5.2 copy-start.1
  406.0 1.1 copy-start.2
  406.1 156.2 %all-gather.4.cloned.1.call-start = ((), (), s32[]{:S(2)}) async-start(), calls=%async_computation.12 | async-start | bytes 6553600 | tf_op jit(solution)/shard_map/all_gather | solution.py:202
  406.1 1.8 copy-start.8
  562.3 6.2 %copy-start = (bf16[2,640,2048]{2,1,0:T(8,128)(2,1)S(1)}, bf16[2,640,2048]{2,1,0:T(8,128)(2,1)}, u32[]{:S(2)}) copy-start(bf16[2,640,2048]{2,1,0:T(8,128)(2,1)} %all-gather.6.cloned.1.call-done) | copy-start | bytes 15728644
  562.3 8.5 %slice-start = ((s8[5242880]{0:T(1024)(128)(4,1)}), s8[4194304]{0:T(1024)(128)(4,1)S(1)}, s32[]{:S(2)}) async-start(s8[5242880]{0:T(1024)(128)(4,1)} %bitcast.17), calls=%async_computation.15 | async-start | bytes 8388608
  568.5 2.4 slice-start.1
Sparse Core Ops, SparseCore 0:
  184.9 32.7 reduce-scatter.6
  220.6 29.6 reduce-scatter.8
  253.2 29.6 reduce-scatter.10
  285.6 29.6 reduce-scatter.12
  317.9 29.6 reduce-scatter.14
  350.3 29.6 reduce-scatter.16
  399.1 52.1 all-gather.7
  453.5 53.2 all-gather.5
  509.0 53.2 all-gather.3
